TPU v7x, 128 devices: a whole 4x4x4 slice. The times are simulated.
128 devices in a mesh: grp: 4 (over y), dev: 32 (over z, x, core).
Axes of the slice: x: 4, y: 4, z: 4, core: 2. Of those that a mesh axis runs over, the one named last changes fastest.
Arguments:
- feeder_state: float32 [12288, 24, 256], P(('grp', 'dev')), may hold values from -6 to 6
- feeder_load: bfloat16 [12288, 24, 256], P(('grp', 'dev')), may hold values from -6 to 6
- feeder_inverse: bfloat16 [12288, 256, 256], P(('grp', 'dev')), as said below
- coupling: bfloat16 [12288, 256], P(('grp', 'dev')), may hold values from -0.375 to 0.375
- feeder_bus: int32 [12288], P(('grp', 'dev')), may hold values from 0 to 16383
- bus_coupling: bfloat16 [16384, 16384], P(('grp', 'dev')), may hold values from -0.09375 to 0.09375
- bus_diagonal: float32 [16384], P(('grp', 'dev')), may hold values from 1 to 3
- bus_load: float32 [24, 16384], P(None, ('grp', 'dev')), may hold values from -6 to 6
- bus_state: float32 [24, 16384], P(None, ('grp', 'dev')), may hold values from -6 to 6
- barrier: float32 [2], replicated, may hold values from 0.5 to 4
- step_length: float32 [2], replicated, may hold values from 0.4 to 1
Outputs:
- feeder_final: float32 [12288, 24, 256], P(('grp', 'dev'))
- bus_final: float32 [24, 16384], P(None, ('grp', 'dev'))
Inputs may be any that keep to these rules, and one draw needn't show every extreme that they name: `feeder_inverse`: each block is symmetric with a positive diagonal and is positive definite.
All inputs are finite; a program needn't handle non-finite values.
Results may differ from a plain program's by a relative error of at most 0.0022.
Values may be sent and summed in bfloat16 or wider, within the bound.
A program may use at most 128 MiB of HBM per device.

v0:
```python
import jax
import jax.numpy as jnp
from jax import lax
from jax.sharding import Mesh
from jax.sharding import PartitionSpec as P

GRP_DEV = ("grp", "dev_0", "dev_1", "dev_2")


def turned_gather(arrays, axis, dims):
    turned = [jnp.moveaxis(a, dim, 0) for a, dim in zip(arrays, dims)]
    widths = [t[0].size for t in turned]
    both = jnp.concatenate([t.reshape(-1, w) for t, w in zip(turned, widths)], axis=1)
    filled = lax.all_gather(both, axis, axis=0, tiled=True)
    blocks = jnp.split(filled, [sum(widths[:k]) for k in range(1, len(widths))], axis=1)
    return tuple(
        (
            jnp.moveaxis(b.reshape(-1, *t.shape[1:]), 0, dim)
            for b, t, dim in zip(blocks, turned, dims)
        )
    )


def from_everyone(array, axis):
    copies = jnp.broadcast_to(array, (lax.axis_size(axis), *array.shape))
    return lax.all_to_all(copies, axis, split_axis=0, concat_axis=0, tiled=True)


def joined_along(blocks, dim):
    blocks = jnp.moveaxis(blocks, 0, dim)
    lengths = blocks.shape
    return blocks.reshape(*lengths[:dim], lengths[dim] * lengths[dim + 1], *lengths[dim + 2 :])


def gather_axes(array, axes, dim):
    far, near = axes
    leading = from_everyone(array, far)
    blocks = jnp.swapaxes(from_everyone(leading, near), 0, 1)
    return joined_along(blocks.reshape(-1, *array.shape), dim)


def on_device(
    feeder_state,
    feeder_load,
    feeder_inverse,
    coupling,
    feeder_bus,
    bus_coupling,
    bus_diagonal,
    bus_load,
    bus_state,
    barrier,
    step_length,
):
    highest = lax.Precision.HIGHEST
    sensitivity = coupling.astype(jnp.float32)
    response = jnp.einsum(
        "fij,fj->fi", feeder_inverse, coupling, preferred_element_type=jnp.float32
    )
    schur = jnp.sum(sensitivity * response, axis=-1)
    bus_local = bus_coupling.shape[0]
    schur_all, buses_all = turned_gather((schur, feeder_bus.astype(jnp.float32)), GRP_DEV, (0, 0))
    bus_first = lax.axis_index(GRP_DEV) * bus_local
    owned = (
        buses_all.astype(jnp.int32)[:, None]
        == bus_first + jnp.arange(bus_local, dtype=jnp.int32)[None, :]
    ).astype(jnp.float32)
    bus_schur = jnp.dot(schur_all, owned, precision=highest)
    feeder_now = feeder_state
    bus_now = bus_state
    for iteration in range(barrier.shape[0]):
        weight_mu = barrier[iteration]
        residual = (
            feeder_load.astype(jnp.float32) + weight_mu * jax.nn.sigmoid(-feeder_now)
        ).astype(jnp.bfloat16)
        solved = jnp.einsum(
            "fij,fhj->fhi", feeder_inverse, residual, preferred_element_type=jnp.float32
        )
        boundary = jnp.sum(solved * sensitivity[:, None, :], axis=-1)
        boundary_all = gather_axes(boundary.T, (("grp", "dev_0", "dev_1"), "dev_2"), 1)
        bus_totals = jnp.dot(boundary_all, owned, precision=highest)
        bus_right = bus_load + weight_mu * jax.nn.sigmoid(-bus_now) - bus_totals
        pivots = bus_diagonal + weight_mu + bus_schur
        first_sweep = (bus_right / pivots).astype(jnp.bfloat16)
        coupled = jnp.einsum(
            "hk,bk->hb",
            gather_axes(first_sweep, (("grp", "dev_0", "dev_1"), "dev_2"), 1),
            bus_coupling,
            preferred_element_type=jnp.float32,
        )
        second_sweep = (bus_right - coupled) / pivots
        bus_now = bus_now + step_length[iteration] * second_sweep
        all_steps = gather_axes(second_sweep, (("grp", "dev_0", "dev_1"), "dev_2"), 1)
        at_feeder = jnp.take(all_steps, feeder_bus, axis=1)
        feeder_now = feeder_now + step_length[iteration] * (
            solved - response[:, None, :] * at_feeder.T[:, :, None]
        )
    return (feeder_now, bus_now)


def solution(mesh):
    split = Mesh(
        mesh.devices.reshape(mesh.shape["grp"], 4, 4, 2), ("grp", "dev_0", "dev_1", "dev_2")
    )
    in_specs = (
        P(GRP_DEV, None, None),
        P(GRP_DEV, None, None),
        P(GRP_DEV, None, None),
        P(GRP_DEV, None),
        P(GRP_DEV),
        P(GRP_DEV, None),
        P(GRP_DEV),
        P(None, GRP_DEV),
        P(None, GRP_DEV),
        P(),
        P(),
    )
    out_specs = (P(GRP_DEV, None, None), P(None, GRP_DEV))
    return jax.shard_map(
        on_device, mesh=split, in_specs=in_specs, out_specs=out_specs, check_vma=False
    )
```

profile of v0, /device:TPU:1, one launch (start us, length us, event | category | flops | bytes accessed | tf_op | source)
XLA Modules:
  0.0 255.7 jit_solution(10424992593101645294)
XLA Ops:
  0.6 1.3 fusion.43
  2.8 11.1 %multiply_reduce_fusion.1 = (f32[96,24]{1,0:T(8,128)S(1)}, f32[96,24,256]{2,1,0:T(8,128)}) fusion(f32[96,256]{1,0:T(8,128)S(1)} %convert_element_type.29, bf16[96,256,256]{2,1,0:T(8,128)(2,1)} %param.15, bf16[96,24,256]{2,1,0:T(8,128)(2,1)} %param.14, f32[96,24,256]{2,1,0:T(8,128)} %param.13, f32[]{:T(128)} %bitcast.1), kind=kOutput, calls=%fused_computation.21 | convolution fusion | flops 306706176 | bytes 18588676 | tf_op jit(solution)/shard_map/fij,fhj->fhi/dot_general | solution.py:76
  13.9 1.0 broadcast_in_dim.57
  14.9 12.0 %all-to-all-start = ((f32[64,24,96]{2,1,0:T(8,128)}), f32[64,24,96]{2,1,0:T(8,128)S(1)}, u32[]{:S(2)}, u32[]{:S(2)}) async-start(f32[64,24,96]{2,1,0:T(8,128)} %broadcast_in_dim.57), calls=%async_computation | async-start | bytes 1572864 | tf_op jit(solution)/shard_map/all_to_all | solution.py:26
  26.9 7.9 %fusion.37 = f32[96,1,256]{2,1,0:T(1,128)S(1)} fusion(bf16[96,256,256]{2,1,0:T(8,128)(2,1)} %param.15, bf16[96,256,1]{1,0,2:T(8,128)(2,1)S(1)} %bitcast.86), kind=kOutput, calls=%fused_computation.40 | convolution fusion | flops 12582912 | bytes 12730368 | tf_op jit(solution)/shard_map/fij,fj->fi/dot_general | solution.py:57
  35.0 36.9 %all-gather = f32[128,96,2]{1,2,0:T(2,128)S(1)} all-gather(f32[1,96,2]{1,2,0:T(2,128)S(1)} %maximum_bitcast_fusion), channel_id=1, replica_groups=mesh['grp'=4,'dev_0'=4,'dev_1'=4,'dev_2'=2] {'grp','dev_0','dev_1','dev_2'}, dimensions={0}, use_global_device_ids=true | all-gather | bytes 99072 | tf_op jit(solution)/shard_map/all_gather | solution.py:14
  72.2 3.9 %add_add_fusion = (f32[128]{0:T(128)S(1)}, f32[128]{0:T(128)S(1)}) fusion(f32[128]{0:T(128)S(1)} %copy-done.7, f32[]{:T(128)} %bitcast.24, f32[]{:T(128)} %bitcast.1, s32[128]{0:T(128)S(1)} %iota_add_fusion, s32[12288]{0:T(1024)S(1)} %bitcast.89, f32[12288,2]{0,1:T(2,128)S(1)} %reshape.100), kind=kOutput, calls=%fused_computation.55 | convolution fusion | flops 20447744 | bytes 100360 | tf_op jit(solution)/shard_map/dot_general | solution.py:68
  76.2 4.8 %all_to_all.60 = f32[2,64,24,96]{3,2,1,0:T(8,128)S(1)} all-to-all(f32[2,64,24,96]{3,2,1,0:T(8,128)S(1)} %broadcast_in_dim.58), channel_id=1, replica_groups=mesh['grp'=4,'dev_0'=4,'dev_1'=4,'dev_2'=2] {'dev_2'}, dimensions={0} | all-to-all | bytes 2359296 | tf_op jit(solution)/shard_map/all_to_all | solution.py:26
  81.5 0.9 reshape.67
  82.4 3.3 %divide_convert_fusion.1 = (bf16[24,128]{1,0:T(8,128)(2,1)S(1)}, f32[24,128]{1,0:T(8,128)S(1)}) fusion(f32[128]{0:T(128)S(1)} %get-tuple-element.4, f32[24,12288]{1,0:T(8,128)S(1)} %reshape.67, s32[128]{0:T(128)S(1)} %iota_add_fusion, s32[12288]{0:T(1024)S(1)} %bitcast.90, f32[24,128]{1,0:T(8,128)S(1)} %copy-done.6, f32[24,128]{1,0:T(8,128)S(1)} %copy-done.3, ...), kind=kOutput, calls=%fused_computation.50 | convolution fusion | flops 454579200 | bytes 1272836 | tf_op jit(solution)/shard_map/dot_general | solution.py:81
  85.8 17.1 %all_to_all.61 = bf16[64,24,128]{2,1,0:T(8,128)(2,1)S(1)} all-to-all(bf16[64,24,128]{2,1,0:T(8,128)(2,1)S(1)} %broadcast_in_dim.59), channel_id=1, replica_groups=mesh['grp'=4,'dev_0'=4,'dev_1'=4,'dev_2'=2] {'grp','dev_0','dev_1'}, dimensions={0} | all-to-all | bytes 786432 | tf_op jit(solution)/shard_map/all_to_all | solution.py:26
  103.0 6.1 %all_to_all.62 = bf16[2,64,24,128]{3,2,1,0:T(8,128)(2,1)S(1)} all-to-all(bf16[2,64,24,128]{3,2,1,0:T(8,128)(2,1)S(1)} %broadcast_in_dim.60), channel_id=1, replica_groups=mesh['grp'=4,'dev_0'=4,'dev_1'=4,'dev_2'=2] {'dev_2'}, dimensions={0} | all-to-all | bytes 1572864 | tf_op jit(solution)/shard_map/all_to_all | solution.py:26
  109.2 1.2 fusion.29
  110.4 1.0 broadcast_in_dim.61
  111.4 4.6 %all-to-all-start.4 = ((f32[64,24,128]{2,1,0:T(8,128)}), f32[64,24,128]{2,1,0:T(8,128)S(1)}, u32[]{:S(2)}, u32[]{:S(2)}) async-start(f32[64,24,128]{2,1,0:T(8,128)} %broadcast_in_dim.61), calls=%async_computation.4 | async-start | bytes 1572864 | tf_op jit(solution)/shard_map/all_to_all | solution.py:26
  116.7 14.9 %all-to-all-done.4 = f32[64,24,128]{2,1,0:T(8,128)S(1)} async-done(((f32[64,24,128]{2,1,0:T(8,128)}), f32[64,24,128]{2,1,0:T(8,128)S(1)}, u32[]{:S(2)}, u32[]{:S(2)}) %all-to-all-start.4) | async-done | bytes 786464 | tf_op jit(solution)/shard_map/all_to_all | solution.py:26
  131.7 6.2 %all_to_all.63 = f32[2,64,24,128]{3,2,1,0:T(8,128)S(1)} all-to-all(f32[2,64,24,128]{3,2,1,0:T(8,128)S(1)} %broadcast_in_dim.62), channel_id=1, replica_groups=mesh['grp'=4,'dev_0'=4,'dev_1'=4,'dev_2'=2] {'dev_2'}, dimensions={0} | all-to-all | bytes 3145728 | tf_op jit(solution)/shard_map/all_to_all | solution.py:26
  138.0 4.6 %copy.42 = f32[24,128,128]{0,2,1:T(8,128)} copy(f32[24,128,128]{2,0,1:T(8,128)S(1)} %bitcast.80) | data formatting | bytes 3145728 | tf_op jit(solution)/shard_map/transpose | solution.py:30
  142.7 4.0 %gather_fusion = f32[96,24]{1,0:T(8,128)S(1)} fusion(f32[24,16384]{0,1:T(8,128)} %bitcast.77, s32[1024]{0:T(1024)S(1)} %pad_clamp_fusion), kind=kCustom, calls=%fused_computation.clone | custom fusion | bytes 18816 | tf_op jit(solution)/shard_map/jit(_take)/gather | solution.py:94
  146.8 12.6 %multiply_reduce_fusion = (f32[96,24]{1,0:T(8,128)S(1)}, f32[96,24,256]{2,1,0:T(8,128)}) fusion(f32[96,256]{1,0:T(8,128)S(1)} %convert_element_type.29, bf16[96,256,256]{2,1,0:T(8,128)(2,1)} %param.15, bf16[96,24,256]{2,1,0:T(8,128)(2,1)S(1)} %copy-done.5, f32[]{:T(128)} %bitcast.24, f32[96,24,256]{2,1,0:T(8,128)} %param.13, ...), kind=kOutput, calls=%fused_computation.19 | convolution fusion | flops 309065472 | bytes 21055496 | tf_op jit(solution)/shard_map/fij,fhj->fhi/dot_general | solution.py:76
  159.5 19.3 %all_to_all.64 = f32[64,24,96]{2,1,0:T(8,128)S(1)} all-to-all(f32[64,24,96]{2,1,0:T(8,128)S(1)} %broadcast_in_dim.63), channel_id=1, replica_groups=mesh['grp'=4,'dev_0'=4,'dev_1'=4,'dev_2'=2] {'grp','dev_0','dev_1'}, dimensions={0} | all-to-all | bytes 1179648 | tf_op jit(solution)/shard_map/all_to_all | solution.py:26
  178.9 6.5 %all_to_all.65 = f32[2,64,24,96]{3,2,1,0:T(8,128)S(1)} all-to-all(f32[2,64,24,96]{3,2,1,0:T(8,128)S(1)} %broadcast_in_dim.64), channel_id=1, replica_groups=mesh['grp'=4,'dev_0'=4,'dev_1'=4,'dev_2'=2] {'dev_2'}, dimensions={0} | all-to-all | bytes 2359296 | tf_op jit(solution)/shard_map/all_to_all | solution.py:26
  185.8 0.9 reshape.76
  186.8 3.8 %divide_convert_fusion = (bf16[24,128]{1,0:T(8,128)(2,1)S(1)}, f32[24,128]{1,0:T(8,128)S(1)}) fusion(f32[128]{0:T(128)S(1)} %get-tuple-element.3, f32[24,12288]{1,0:T(8,128)S(1)} %reshape.76, s32[128]{0:T(128)S(1)} %iota_add_fusion, s32[12288]{0:T(1024)S(1)} %bitcast.91, f32[24,128]{1,0:T(8,128)S(1)} %copy-done.6, f32[24,128]{1,0:T(8,128)S(1)} %copy-done.3, ...), kind=kOutput, calls=%fused_computation.48 | convolution fusion | flops 454585344 | bytes 1285128 | tf_op jit(solution)/shard_map/dot_general | solution.py:81
  190.6 15.2 %all_to_all.66 = bf16[64,24,128]{2,1,0:T(8,128)(2,1)S(1)} all-to-all(bf16[64,24,128]{2,1,0:T(8,128)(2,1)S(1)} %broadcast_in_dim.65), channel_id=1, replica_groups=mesh['grp'=4,'dev_0'=4,'dev_1'=4,'dev_2'=2] {'grp','dev_0','dev_1'}, dimensions={0} | all-to-all | bytes 786432 | tf_op jit(solution)/shard_map/all_to_all | solution.py:26
  205.9 6.1 %all_to_all.67 = bf16[2,64,24,128]{3,2,1,0:T(8,128)(2,1)S(1)} all-to-all(bf16[2,64,24,128]{3,2,1,0:T(8,128)(2,1)S(1)} %broadcast_in_dim.66), channel_id=1, replica_groups=mesh['grp'=4,'dev_0'=4,'dev_1'=4,'dev_2'=2] {'dev_2'}, dimensions={0} | all-to-all | bytes 1572864 | tf_op jit(solution)/shard_map/all_to_all | solution.py:26
  212.1 2.9 %multiply_add_fusion.3 = (f32[24,128]{1,0:T(8,128)}, f32[24,128]{1,0:T(8,128)S(1)}) fusion(f32[]{:T(128)} %bitcast.23, f32[24,128]{1,0:T(8,128)S(1)} %copy-done.3, f32[24,128]{1,0:T(8,128)S(1)} %fusion.29, f32[]{:T(128)} %bitcast, f32[128]{0:T(128)S(1)} %get-tuple-element.3, f32[24,128]{1,0:T(8,128)S(1)} %get-tuple-element.18, ...), kind=kOutput, calls=%fused_computation.47 | convolution fusion | flops 100681728 | bytes 5042696 | tf_op jit(solution)/shard_map/hk,bk->hb/dot_general | solution.py:85
  215.1 19.5 %all_to_all.68 = f32[64,24,128]{2,1,0:T(8,128)S(1)} all-to-all(f32[64,24,128]{2,1,0:T(8,128)S(1)} %broadcast_in_dim.67), channel_id=1, replica_groups=mesh['grp'=4,'dev_0'=4,'dev_1'=4,'dev_2'=2] {'grp','dev_0','dev_1'}, dimensions={0} | all-to-all | bytes 1572864 | tf_op jit(solution)/shard_map/all_to_all | solution.py:26
  234.7 6.5 %all_to_all.69 = f32[2,64,24,128]{3,2,1,0:T(8,128)S(1)} all-to-all(f32[2,64,24,128]{3,2,1,0:T(8,128)S(1)} %broadcast_in_dim.68), channel_id=1, replica_groups=mesh['grp'=4,'dev_0'=4,'dev_1'=4,'dev_2'=2] {'dev_2'}, dimensions={0} | all-to-all | bytes 3145728 | tf_op jit(solution)/shard_map/all_to_all | solution.py:26
  241.4 4.6 %copy.49 = f32[24,128,128]{0,2,1:T(8,128)} copy(f32[24,128,128]{2,0,1:T(8,128)S(1)} %bitcast.83) | data formatting | bytes 3145728 | tf_op jit(solution)/shard_map/transpose | solution.py:30
  246.0 4.0 %gather_fusion.1 = f32[96,24]{1,0:T(8,128)S(1)} fusion(f32[24,16384]{0,1:T(8,128)} %bitcast.76, s32[1024]{0:T(1024)S(1)} %pad_clamp_fusion), kind=kCustom, calls=%fused_computation.1.clone | custom fusion | bytes 18816 | tf_op jit(solution)/shard_map/jit(_take)/gather | solution.py:94
  250.1 5.6 %multiply_add_fusion = f32[96,24,256]{2,1,0:T(8,128)} fusion(f32[96,24,256]{2,1,0:T(8,128)} %get-tuple-element.16, f32[96,24]{1,0:T(8,128)S(1)} %broadcast_select_fusion, f32[]{:T(128)} %bitcast.23, f32[96,256]{1,0:T(8,128)S(1)} %bitcast.88, f32[96,24,256]{2,1,0:T(8,128)} %param.13, f32[96,24,256]{2,1,0:T(8,128)} %get-tuple-element.12, ...), kind=kLoop, calls=%fused_computation.18 | loop fusion | flops 4718592 | bytes 9553928 | tf_op jit(solution)/shard_map/add | solution.py:95
  (53 shorter events, 4.2 us)
Async XLA Ops:
  13.9 13.0 %copy-start.8 = (s32[96]{0:T(128)S(1)}, s32[96]{0:T(128)}, u32[]{:S(2)}) copy-start(s32[96]{0:T(128)} %param.17) | copy-start | bytes 1156
  13.9 13.0 %copy-start.2 = (bf16[96,256]{1,0:T(8,128)(2,1)S(1)}, bf16[96,256]{1,0:T(8,128)(2,1)}, u32[]{:S(2)}) copy-start(bf16[96,256]{1,0:T(8,128)(2,1)} %param.16) | copy-start | bytes 147460
  14.9 61.2 %all-to-all-start = ((f32[64,24,96]{2,1,0:T(8,128)}), f32[64,24,96]{2,1,0:T(8,128)S(1)}, u32[]{:S(2)}, u32[]{:S(2)}) async-start(f32[64,24,96]{2,1,0:T(8,128)} %broadcast_in_dim.57), calls=%async_computation | async-start | bytes 1572864 | tf_op jit(solution)/shard_map/all_to_all | solution.py:26
  26.9 45.3 %copy-start.7 = (f32[128]{0:T(128)S(1)}, f32[128]{0:T(128)}, u32[]{:S(2)}) copy-start(f32[128]{0:T(128)} %param.19) | copy-start | bytes 1540
  81.2 1.2 copy-start.3
  81.2 1.2 copy-start.6
  102.9 6.3 %copy-start = (bf16[128,16384]{1,0:T(8,128)(2,1)S(1)}, bf16[128,16384]{1,0:T(8,128)(2,1)}, u32[]{:S(2)}) copy-start(bf16[128,16384]{1,0:T(8,128)(2,1)} %param.18) | copy-start | bytes 12582916
  110.4 5.7 %copy-start.4 = (f32[2]{0:T(128)S(1)}, f32[2]{0:T(128)}, u32[]{:S(2)}) copy-start(f32[2]{0:T(128)} %param.23) | copy-start | bytes 28
  111.4 20.2 %all-to-all-start.4 = ((f32[64,24,128]{2,1,0:T(8,128)}), f32[64,24,128]{2,1,0:T(8,128)S(1)}, u32[]{:S(2)}, u32[]{:S(2)}) async-start(f32[64,24,128]{2,1,0:T(8,128)} %broadcast_in_dim.61), calls=%async_computation.4 | async-start | bytes 1572864 | tf_op jit(solution)/shard_map/all_to_all | solution.py:26
  138.0 8.7 %copy-start.5 = (bf16[96,24,256]{2,1,0:T(8,128)(2,1)S(1)}, bf16[96,24,256]{2,1,0:T(8,128)(2,1)}, u32[]{:S(2)}) copy-start(bf16[96,24,256]{2,1,0:T(8,128)(2,1)} %param.14) | copy-start | bytes 3538948
  205.8 6.3 %copy-start.1 = (bf16[128,16384]{1,0:T(8,128)(2,1)S(1)}, bf16[128,16384]{1,0:T(8,128)(2,1)}, u32[]{:S(2)}) copy-start(bf16[128,16384]{1,0:T(8,128)(2,1)} %param.18) | copy-start | bytes 12582916
where the time goes:
time: 257 us; the launch traced here: 256 us
  blocking collectives  144 us (56%)
  matrix products  46.7 us (18%)
  local copies, waits for them, and re-layouts  25.3 us (10%)
  starting transfers between devices  16.6 us (6%)
  waiting for transfers between devices  14.9 us (6%)
  other arithmetic  6.78 us (3%)
    all_to_all x10, blocking collectives, from_everyone(): return lax.all_to_all(copies, axis, split_axis=0, concat_axis=0, tiled=True)  107 us
    all_gather x1, blocking collectives, turned_gather(): filled = lax.all_gather(both, axis, axis=0, tiled=True)  36.9 us
    dot_general x2, matrix products, on_device(): jnp.einsum('fij,fhj->fhi', feeder_inverse, residual, preferred_element_ty...  23.7 us
    all_to_all x2, starting transfers between devices, from_everyone(): return lax.all_to_all(copies, axis, split_axis=0, concat_axis=0, tiled=True)  16.6 us
    all_to_all x2, waiting for transfers between devices, from_everyone(): return lax.all_to_all(copies, axis, split_axis=0, concat_axis=0, tiled=True)  14.9 us
    transpose x4, local copies, waits for them, and re-layouts, joined_along(): blocks = jnp.moveaxis(blocks, 0, dim)  9.86 us
    gather x2, local copies, waits for them, and re-layouts, on_device(): at_feeder = jnp.take(all_steps, feeder_bus, axis=1)  8 us
    dot_general x1, matrix products, on_device(): jnp.einsum('fij,fj->fi', feeder_inverse, coupling, preferred_element_type...  7.91 us
  transfers between devices with their start and end apart: 2, of which 1 were waited for; matrix products, arithmetic and copies ran while one was open for 5% of the time, Pallas kernels for 0%

commit v1 on v0

v1 whole, which is shorter than its diff:
```python
import functools

import jax
import jax.numpy as jnp
from jax import lax
from jax.experimental import pallas as pl
from jax.experimental.pallas import tpu as pltpu
from jax.sharding import PartitionSpec as P

MESH = pl.DeviceIdType.MESH
BOTH = ("grp", "dev")
LANES = 128
CHUNK = 8

OFFSETS = sorted(
    [(a, b, c) for a in range(4) for b in range(4) for c in range(4) if a or b or c],
    key=lambda t: -sum(min(v, 4 - v) for v in t),
)
GROUPS = (0, 1, 3, 2)


def place():
    y, d = lax.axis_index("grp"), lax.axis_index("dev")
    return y, d // 8, (d // 2) % 4, d % 2


def device(y, z, x, c):
    return (y, z * 8 + x * 2 + c)


def chip_of(y, z, x):
    return (y * 4 + z) * 4 + x


def plane_of(plane, count=16):
    return pl.ds(plane * 16, count)


def announce():
    y, z, x, c = place()
    bar = pltpu.get_barrier_semaphore()
    for dy, dz, dx in OFFSETS:
        to = device((y + dy) % 4, (z + dz) % 4, (x + dx) % 4, c)
        pl.semaphore_signal(bar, inc=1, device_id=to, device_id_type=MESH)
    pl.semaphore_signal(bar, inc=1, device_id=device(y, z, x, 1 - c), device_id_type=MESH)


def all_here():
    pl.semaphore_wait(pltpu.get_barrier_semaphore(), len(OFFSETS) + 1)


def send(buf, sems):
    sent, came, _, _ = sems
    y, z, x, c = place()
    for dy, dz, dx in OFFSETS:
        pltpu.make_async_remote_copy(
            src_ref=buf.at[c, chip_of(y, z, x)],
            dst_ref=buf.at[c, chip_of(y, z, x)],
            send_sem=sent,
            recv_sem=came.at[dy],
            device_id=device((y + dy) % 4, (z + dz) % 4, (x + dx) % 4, c),
            device_id_type=MESH,
        ).start()


def bytes_of(ref, sem):
    pltpu.make_async_copy(ref, ref, sem).wait()


def pass_on(buf, sems, dy):
    _, came, handed, _ = sems
    y, z, x, c = place()
    plane = (y + 4 - dy) % 4
    bytes_of(buf.at[c, plane_of(plane, 16 if dy else 15)], came.at[dy])
    pltpu.make_async_remote_copy(
        src_ref=buf.at[c, plane_of(plane)],
        dst_ref=buf.at[c, plane_of(plane)],
        send_sem=handed,
        recv_sem=sems[3].at[dy],
        device_id=device(y, z, x, 1 - c),
        device_id_type=MESH,
    ).start()


def partner_came(buf, sems, dy):
    y, z, x, c = place()
    plane = (y + 4 - dy) % 4
    bytes_of(buf.at[1 - c, plane_of(plane)], sems[3].at[dy])
    return plane


def drained(buf, sems):
    sent, _, handed, _ = sems
    c = place()[3]
    bytes_of(buf.at[c, 0 : len(OFFSETS)], sent)
    bytes_of(buf.at[c], handed)


def plane_rows(buf, plane, tail=None):
    blocks = []
    for k in range(16):
        for c in range(2):
            block = buf[c, plane * 16 + k]
            if tail is not None:
                block = jnp.concatenate([block, tail(c, plane * 16 + k)], axis=0)
            blocks.append(block)
    return jnp.concatenate(blocks, axis=1)


def gather_dot(buf, sems, weights, tail=None):
    total = None

    def product(dy):
        plane = partner_came(buf, sems, dy)
        columns = pl.ds(pl.multiple_of(plane * (32 * LANES), LANES), 32 * LANES)
        return lax.dot_general(
            plane_rows(buf, plane, tail),
            weights[:, columns],
            (((1,), (1,)), ((), ())),
            preferred_element_type=jnp.float32,
        )

    for k, dy in enumerate(GROUPS):
        pass_on(buf, sems, dy)
        if k:
            part = product(GROUPS[k - 1])
            total = part if total is None else total + part
    return total + product(GROUPS[-1])


def kernel(
    state_hbm,
    load_hbm,
    inverse_hbm,
    coupling_ref,
    bus_ref,
    network_hbm,
    diagonal_ref,
    bus_load_ref,
    bus_state_ref,
    barrier_ref,
    step_ref,
    y_hbm,
    response_ref,
    at_ref,
    bus_final_ref,
    inverse,
    state,
    load,
    solved,
    network,
    owned,
    chosen,
    sensitivity,
    blocks,
    schur_all,
    ids_all,
    load_sems,
    out_sem,
    sent,
    came,
    handed,
    partner,
):
    feeders = state.shape[0]
    chunks = feeders // CHUNK
    hours = state.shape[1]
    y, z, x, c = place()
    chip = chip_of(y, z, x)
    me = chip * 2 + c

    def chunk_copies(k):
        at = pl.ds(k * CHUNK, CHUNK)
        return [
            pltpu.make_async_copy(inverse_hbm.at[at], inverse.at[at], load_sems.at[0, k]),
            pltpu.make_async_copy(state_hbm.at[at], state.at[at], load_sems.at[1, k]),
            pltpu.make_async_copy(load_hbm.at[at], load.at[at], load_sems.at[2, k]),
        ]

    @pl.loop(0, chunks)
    def _(k):
        for copy in chunk_copies(k):
            copy.start()

    network_copy = pltpu.make_async_copy(network_hbm, network, load_sems.at[3, 0])
    network_copy.start()
    announce()

    def sems(p):
        return sent.at[p], came.at[p], handed.at[p], partner.at[p]

    sensitivity[...] = coupling_ref[...].astype(jnp.float32)
    lane = lax.broadcasted_iota(jnp.int32, (hours + 8, LANES), 1)

    mu = barrier_ref[0]

    def first_chunk(k, edge):
        for copy in chunk_copies(k):
            copy.wait()
        start = pl.multiple_of(k * CHUNK, CHUNK)
        rows = sensitivity[pl.ds(start, CHUNK), :]
        responses = []
        for j in range(CHUNK):
            f = start + j
            row = rows[j : j + 1, :]
            right = load[f].astype(jnp.float32) + mu * jax.nn.sigmoid(-state[f])
            right = jnp.concatenate([right, jnp.broadcast_to(row, (8, row.shape[1]))], axis=0)
            product = jnp.dot(
                right.astype(jnp.bfloat16), inverse[f], preferred_element_type=jnp.float32
            )
            solved[f] = product[:hours]
            responses.append(product[hours : hours + 1])
            scaled = product * row
            term = jnp.sum(scaled[:, :LANES] + scaled[:, LANES:], axis=1, keepdims=True)
            edge = jnp.where(lane == f, term, edge)
        response_ref[pl.ds(start, CHUNK), :] = jnp.concatenate(responses, axis=0)
        return edge

    edge = lax.fori_loop(0, chunks, first_chunk, jnp.zeros((hours + 8, LANES), jnp.float32))

    own = (c, chip)
    all_here()
    ids_all[own] = jnp.full((1, LANES), -1, jnp.int32)
    ids_all[c, chip, :, 0:feeders] = bus_ref[...]
    send(ids_all, sems(0))
    schur_all[own] = edge[hours : hours + 1]
    send(schur_all, sems(1))
    blocks[0, c, chip] = edge[:hours].astype(jnp.bfloat16)
    send(blocks.at[0], sems(2))

    for dy in GROUPS:
        pass_on(ids_all, sems(0), dy)
    for dy in GROUPS:
        partner_came(ids_all, sems(0), dy)
    my_bus = me * LANES + lax.broadcasted_iota(jnp.int32, (LANES, LANES), 0)

    @pl.loop(0, 64)
    def _(k):
        for core in range(2):
            ids = ids_all[core, k]
            columns = pl.ds(pl.multiple_of((k * 2 + core) * LANES, LANES), LANES)
            owned[:, columns] = jnp.where(my_bus == ids, 1.0, 0.0).astype(jnp.bfloat16)

    for dy in GROUPS:
        pass_on(schur_all, sems(1), dy)
    for dy in GROUPS:
        partner_came(schur_all, sems(1), dy)
    row8 = lax.broadcasted_iota(jnp.int32, (8, LANES), 0)

    def schur_rows(core, k):
        whole = jnp.broadcast_to(schur_all[core, k], (8, LANES))
        high = whole.astype(jnp.bfloat16).astype(jnp.float32)
        rows = jnp.where(row8 == 0, high, jnp.where(row8 == 1, whole - high, 0.0))
        return rows.astype(jnp.bfloat16)

    totals = gather_dot(blocks.at[0], sems(2), owned, schur_rows)
    bus_schur = totals[hours : hours + 1] + totals[hours + 1 : hours + 2]
    totals = totals[:hours]

    def bus_phase(totals, mu, step, bus_now, p):
        right = bus_load_ref[...] + mu * jax.nn.sigmoid(-bus_now) - totals
        pivots = diagonal_ref[...] + mu + bus_schur
        blocks[p, c, chip] = (right / pivots).astype(jnp.bfloat16)
        send(blocks.at[p], sems(p + 2))
        if p == 1:
            network_copy.wait()
        coupled = gather_dot(blocks.at[p], sems(p + 2), network)
        second = (right - coupled) / pivots
        blocks[p + 1, c, chip] = second.astype(jnp.bfloat16)
        send(blocks.at[p + 1], sems(p + 3))
        return bus_now + step * second

    bus_now = bus_phase(totals, mu, step_ref[0], bus_state_ref[...], 1)

    my_ids = jnp.broadcast_to(ids_all[own], (LANES, LANES)).T
    along = lax.broadcasted_iota(jnp.int32, (LANES, LANES), 1)

    @pl.loop(0, 128)
    def _(k):
        columns = pl.ds(pl.multiple_of(k * LANES, LANES), LANES)
        chosen[:, columns] = jnp.where(my_ids == along + k * LANES, 1.0, 0.0).astype(jnp.bfloat16)

    at = step_ref[0] * gather_dot(blocks.at[2], sems(4), chosen)

    mu = barrier_ref[1]
    step = step_ref[0]

    def second_chunk(k, edge):
        start = pl.multiple_of(k * CHUNK, CHUNK)
        rows = response_ref[pl.ds(start, CHUNK), :]
        here = pltpu.roll(at, lax.rem(LANES - start, LANES), 1)
        for j in range(CHUNK):
            f = start + j
            row = rows[j : j + 1, :]
            now = state[f] + (step * solved[f] - row * here[:, j : j + 1])
            state[f] = now
            residual = (load[f].astype(jnp.float32) + mu * jax.nn.sigmoid(-now)).astype(jnp.bfloat16)
            load[f] = residual
            scaled = residual.astype(jnp.float32) * row
            term = jnp.sum(scaled[:, :LANES] + scaled[:, LANES:], axis=1, keepdims=True)
            edge = jnp.where(lane[:hours] == f, term, edge)
        return edge

    edge = lax.fori_loop(0, chunks, second_chunk, jnp.zeros((hours, LANES), jnp.float32))
    blocks[3, c, chip] = edge.astype(jnp.bfloat16)
    send(blocks.at[3], sems(5))

    def y_copy(k):
        at = pl.ds(k * CHUNK, CHUNK)
        return pltpu.make_async_copy(solved.at[at], y_hbm.at[at], out_sem.at[k])

    last_step = step_ref[1]

    @pl.loop(0, chunks)
    def _(k):
        for j in range(CHUNK):
            f = k * CHUNK + j
            product = jnp.dot(load[f], inverse[f], preferred_element_type=jnp.float32)
            solved[f] = state[f] + last_step * product
        y_copy(k).start()

    totals = gather_dot(blocks.at[3], sems(5), owned)
    bus_final_ref[...] = bus_phase(totals, mu, last_step, bus_now, 4)
    at_ref[...] = last_step * gather_dot(blocks.at[5], sems(7), chosen)

    @pl.loop(0, chunks)
    def _(k):
        y_copy(k).wait()

    drained(ids_all, sems(0))
    drained(schur_all, sems(1))
    for p in range(6):
        drained(blocks.at[p], sems(p + 2))


def on_device(
    feeder_state,
    feeder_load,
    feeder_inverse,
    coupling,
    feeder_bus,
    bus_coupling,
    bus_diagonal,
    bus_load,
    bus_state,
    barrier,
    step_length,
):
    feeders, hours, nodes = feeder_state.shape
    owned, buses = bus_coupling.shape
    f32, bf16 = jnp.float32, jnp.bfloat16
    vmem, smem = pl.BlockSpec(memory_space=pltpu.VMEM), pl.BlockSpec(memory_space=pltpu.SMEM)
    hbm = pl.BlockSpec(memory_space=pl.ANY)
    chunks = feeders // CHUNK
    y, response, at, bus_final = pl.pallas_call(
        kernel,
        name="interior_point",
        out_shape=[
            jax.ShapeDtypeStruct((feeders, hours, nodes), f32),
            jax.ShapeDtypeStruct((feeders, nodes), f32),
            jax.ShapeDtypeStruct((hours, LANES), f32),
            jax.ShapeDtypeStruct((hours, owned), f32),
        ],
        in_specs=[hbm, hbm, hbm, vmem, vmem, hbm, vmem, vmem, vmem, smem, smem],
        out_specs=[hbm, vmem, vmem, vmem],
        scratch_shapes=[
            pltpu.VMEM((feeders, nodes, nodes), bf16),
            pltpu.VMEM((feeders, hours, nodes), f32),
            pltpu.VMEM((feeders, hours, nodes), bf16),
            pltpu.VMEM((feeders, hours, nodes), f32),
            pltpu.VMEM((owned, buses), bf16),
            pltpu.VMEM((LANES, 128 * LANES), bf16),
            pltpu.VMEM((LANES, buses), bf16),
            pltpu.VMEM((feeders, nodes), f32),
            pltpu.VMEM((6, 2, 64, hours, LANES), bf16),
            pltpu.VMEM((2, 64, 1, LANES), f32),
            pltpu.VMEM((2, 64, 1, LANES), jnp.int32),
            pltpu.SemaphoreType.DMA((4, chunks)),
            pltpu.SemaphoreType.DMA((chunks,)),
            pltpu.SemaphoreType.DMA((8,)),
            pltpu.SemaphoreType.DMA((8, 4)),
            pltpu.SemaphoreType.DMA((8,)),
            pltpu.SemaphoreType.DMA((8, 4)),
        ],
        compiler_params=pltpu.CompilerParams(
            collective_id=0, has_side_effects=True, vmem_limit_bytes=60 * 2**20
        ),
    )(
        feeder_state,
        feeder_load,
        feeder_inverse,
        coupling,
        feeder_bus.reshape(1, feeders),
        bus_coupling,
        bus_diagonal.reshape(1, owned),
        bus_load,
        bus_state,
        barrier,
        step_length,
    )
    at_feeder = at[:, :feeders].T
    return y - response[:, None, :] * at_feeder[:, :, None], bus_final


def solution(mesh):
    in_specs = (
        P(BOTH, None, None),
        P(BOTH, None, None),
        P(BOTH, None, None),
        P(BOTH, None),
        P(BOTH),
        P(BOTH, None),
        P(BOTH),
        P(None, BOTH),
        P(None, BOTH),
        P(),
        P(),
    )
    out_specs = (P(BOTH, None, None), P(None, BOTH))
    return jax.shard_map(
        on_device, mesh=mesh, in_specs=in_specs, out_specs=out_specs, check_vma=False
    )
```

time: 257 us -> 93.3 us (0.36)
  blocking collectives: 144 us -> 0 us
  Pallas kernels: 0 us -> 87.5 us
  matrix products: 46.7 us -> 0 us
  local copies, waits for them, and re-layouts: 25.3 us -> 1.4 us
  starting transfers between devices: 16.6 us -> 0 us
  waiting for transfers between devices: 14.9 us -> 0 us
  other arithmetic: 6.78 us -> 3.46 us
    all_to_all x10 -> x0, blocking collectives: 107 us -> none  [from_everyone(): return lax.all_to_all(copies, axis, split_axis=0, concat_axis=0, tiled=True)]
    pallas_call x0 -> x1, Pallas kernels: none -> 87.5 us  [on_device(): pl.pallas_call(kernel, name='interior_point', out_shape=[jax.ShapeDtypeSt...]
    dot_general x8 -> x0, matrix products: 46.7 us -> none  [the longest x2 23.7 us: on_device(): jnp.einsum('fij,fhj->fhi', feeder_inverse, residual, preferred_element_ty...]
    all_gather x1 -> x0, blocking collectives: 36.9 us -> none  [turned_gather(): filled = lax.all_gather(both, axis, axis=0, tiled=True)]
    all_to_all x2 -> x0, starting transfers between devices: 16.6 us -> none  [from_everyone(): return lax.all_to_all(copies, axis, split_axis=0, concat_axis=0, tiled=True)]
    all_to_all x2 -> x0, waiting for transfers between devices: 14.9 us -> none  [from_everyone(): return lax.all_to_all(copies, axis, split_axis=0, concat_axis=0, tiled=True)]
    transpose x8 -> x2, local copies, waits for them, and re-layouts: 10.2 us -> 0.8 us  [on_device(): at_feeder = at[:, :feeders].T]
    gather x2 -> x0, local copies, waits for them, and re-layouts: 8 us -> none  [on_device(): at_feeder = jnp.take(all_steps, feeder_bus, axis=1)]
  transfers between devices with their start and end apart: 2 -> 0, of which waited for: 1 -> 0; matrix products, arithmetic and copies ran while one was open for 5% -> 0% of each run, Pallas kernels for 0% -> 0%
where the time goes in v1:
time: 93.3 us; the launch traced here: 93 us
  Pallas kernels  87.5 us (94%)
  other arithmetic  3.46 us (4%)
  local copies, waits for them, and re-layouts  1.4 us (2%)
    pallas_call x1, Pallas kernels, on_device(): pl.pallas_call(kernel, name='interior_point', out_shape=[jax.ShapeDtypeSt...  87.5 us
    sub x1, other arithmetic, on_device(): return (y - response[:, None, :] * at_feeder[:, :, None], bus_final)  3.46 us

profile of v1, /device:TPU:1, one launch (start us, length us, event | category | flops | bytes accessed | tf_op | source)
XLA Modules:
  0.0 93.0 jit_solution(519922166191037543)
XLA Ops:
  0.6 87.5 %interior_point.1 = (f32[96,24,256]{2,1,0:T(8,128)}, f32[96,256]{1,0:T(8,128)}, f32[24,128]{1,0:T(8,128)}, f32[24,128]{1,0:T(8,128)}) custom-call(f32[96,24,256]{2,1,0:T(8,128)} %state_hbm.1, bf16[96,24,256]{2,1,0:T(8,128)(2,1)} %load_hbm.1, bf16[96,256,256]{2,1,0:T(8,128)(2,1)} %inverse_hbm.1, bf16[96,256]{1,0:T(8,128)(2,1)} %coupling_ref.1, ...), custom_call_target="tpu_custom_call" | custom-call | tf_op jit(solution)/shard_map/interior_point/pallas_call | solution.py:355
  88.2 0.7 slice_bitcast_fusion
  88.9 0.1 copy.13
  89.0 0.0 copy-start
  89.0 3.5 %multiply_subtract_fusion = f32[96,24,256]{2,1,0:T(8,128)} fusion(f32[96,24,256]{2,1,0:T(8,128)} %get-tuple-element.6, f32[96,24]{1,0:T(8,128)S(1)} %copy.13, f32[96,256]{1,0:T(8,128)} %get-tuple-element.7), kind=kLoop, calls=%fused_computation | loop fusion | flops 1179648 | bytes 4826112 | tf_op jit(solution)/shard_map/sub | solution.py:402
  92.4 0.0 copy-done
  92.4 0.6 copy.15
Async XLA Ops:
  89.0 3.5 %copy-start = (f32[24,128]{1,0:T(8,128)S(1)}, f32[24,128]{1,0:T(8,128)}, u32[]{:S(2)}) copy-start(f32[24,128]{1,0:T(8,128)} %get-tuple-element.13) | copy-start | bytes 36868

commit v2 on v1

v2 whole, which is shorter than its diff:
```python
import functools

import jax
import jax.numpy as jnp
from jax import lax
from jax.experimental import pallas as pl
from jax.experimental.pallas import tpu as pltpu
from jax.sharding import PartitionSpec as P

MESH = pl.DeviceIdType.MESH
BOTH = ("grp", "dev")
LANES = 128
CHUNK = 8
AHEAD = 4

OFFSETS = sorted(
    [(a, b, c) for a in range(4) for b in range(4) for c in range(4) if a or b or c],
    key=lambda t: -sum(min(v, 4 - v) for v in t),
)
GROUPS = (0, 1, 3, 2)


def place():
    y, d = lax.axis_index("grp"), lax.axis_index("dev")
    return y, d // 8, (d // 2) % 4, d % 2


def device(y, z, x, c):
    return (y, z * 8 + x * 2 + c)


def chip_of(y, z, x):
    return (y * 4 + z) * 4 + x


def plane_of(plane, count=16):
    return pl.ds(plane * 16, count)


def announce():
    y, z, x, c = place()
    bar = pltpu.get_barrier_semaphore()
    for dy, dz, dx in OFFSETS:
        to = device((y + dy) % 4, (z + dz) % 4, (x + dx) % 4, c)
        pl.semaphore_signal(bar, inc=1, device_id=to, device_id_type=MESH)
    pl.semaphore_signal(bar, inc=1, device_id=device(y, z, x, 1 - c), device_id_type=MESH)


def all_here():
    pl.semaphore_wait(pltpu.get_barrier_semaphore(), len(OFFSETS) + 1)


def send(buf, sems):
    y, z, x, c = place()
    chip = chip_of(y, z, x)
    for dy, dz, dx in OFFSETS:
        pltpu.make_async_remote_copy(
            src_ref=buf.at[chip],
            dst_ref=buf.at[chip],
            send_sem=sems[0],
            recv_sem=sems[1].at[dy],
            device_id=device((y + dy) % 4, (z + dz) % 4, (x + dx) % 4, c),
            device_id_type=MESH,
        ).start()


def bytes_of(ref, sem):
    pltpu.make_async_copy(ref, ref, sem).wait()


def came(buf, sems, dy):
    plane = (place()[0] + 4 - dy) % 4
    bytes_of(buf.at[plane_of(plane, 16 if dy else 15)], sems[1].at[dy])
    return plane


def to_partner(src, dst, send_sem, recv_sem):
    y, z, x, c = place()
    return pltpu.make_async_remote_copy(
        src_ref=src,
        dst_ref=dst,
        send_sem=send_sem,
        recv_sem=recv_sem,
        device_id=device(y, z, x, 1 - c),
        device_id_type=MESH,
    )


def gather_dot(buf, sems, weights, theirs, ours):
    total = None
    for dy in GROUPS:
        plane = came(buf, sems, dy)
        columns = pl.ds(pl.multiple_of(plane * (16 * LANES), LANES), 16 * LANES)
        part = lax.dot_general(
            jnp.concatenate([buf[plane * 16 + k] for k in range(16)], axis=1),
            weights[:, columns],
            (((1,), (1,)), ((), ())),
            preferred_element_type=jnp.float32,
        )
        total = part if total is None else total + part
    rows = total.shape[0]
    theirs[0:rows] = total[:, LANES:]
    copy = to_partner(theirs.at[0:rows], ours.at[0:rows], sems[2], sems[3])
    copy.start()
    copy.wait()
    return total[:, :LANES] + ours[0:rows]


def kernel(
    state_hbm,
    load_hbm,
    inverse_hbm,
    coupling_ref,
    bus_ref,
    network_hbm,
    diagonal_ref,
    bus_load_ref,
    bus_state_ref,
    barrier_ref,
    step_ref,
    y_ref,
    response_ref,
    at_ref,
    bus_final_ref,
    inverse,
    state,
    load,
    solved,
    network,
    owned,
    chosen,
    sensitivity,
    blocks0,
    blocks,
    ids_all,
    my_ids,
    their_ids,
    theirs,
    ours,
    load_sems,
    net_sems,
    sent,
    arrived,
    half_sent,
    half_came,
):
    feeders = state.shape[0]
    chunks = feeders // CHUNK
    hours = state.shape[1]
    y, z, x, c = place()
    chip = chip_of(y, z, x)

    def chunk_copies(k):
        at = pl.ds(k * CHUNK, CHUNK)
        return [
            pltpu.make_async_copy(inverse_hbm.at[at], inverse.at[at], load_sems.at[0, k]),
            pltpu.make_async_copy(state_hbm.at[at], state.at[at], load_sems.at[1, k]),
            pltpu.make_async_copy(load_hbm.at[at], load.at[at], load_sems.at[2, k]),
        ]

    def start(k):
        for copy in chunk_copies(k):
            copy.start()

    for k in range(AHEAD):
        start(k)
    announce()

    def block_columns(k, core):
        return pl.ds(pl.multiple_of((k * 2 + core) * LANES, LANES), LANES)

    def columns_of(k):
        return pl.ds(pl.multiple_of(k * LANES, LANES), LANES)

    def sems(p):
        return sent.at[p], arrived.at[p], half_sent.at[p], half_came.at[p]

    sensitivity[...] = coupling_ref[...].astype(jnp.float32)
    lane = lax.broadcasted_iota(jnp.int32, (hours + 8, LANES), 1)

    mu = barrier_ref[0]

    def first_chunk(k, edge):
        for copy in chunk_copies(k):
            copy.wait()
        start = pl.multiple_of(k * CHUNK, CHUNK)
        rows = sensitivity[pl.ds(start, CHUNK), :]
        responses = []
        for j in range(CHUNK):
            f = start + j
            row = rows[j : j + 1, :]
            right = load[f].astype(jnp.float32) + mu * jax.nn.sigmoid(-state[f])
            right = jnp.concatenate([right, jnp.broadcast_to(row, (8, row.shape[1]))], axis=0)
            product = jnp.dot(
                right.astype(jnp.bfloat16), inverse[f], preferred_element_type=jnp.float32
            )
            solved[f] = product[:hours]
            responses.append(product[hours : hours + 1])
            scaled = product * row
            term = jnp.sum(scaled[:, :LANES] + scaled[:, LANES:], axis=1, keepdims=True)
            edge = jnp.where(lane == f, term, edge)
        response_ref[pl.ds(start, CHUNK), :] = jnp.concatenate(responses, axis=0)
        return edge

    def first_with_next(k, edge):
        start(k + AHEAD)
        return first_chunk(k, edge)

    edge = lax.fori_loop(
        0, chunks - AHEAD, first_with_next, jnp.zeros((hours + 8, LANES), jnp.float32)
    )

    all_here()
    my_ids[...] = jnp.full((1, LANES), -1, jnp.int32)
    my_ids[:, 0:feeders] = bus_ref[...]
    ids_all[chip] = my_ids[...]
    send(ids_all, sems(0))
    ids_copy = to_partner(my_ids, their_ids, half_sent.at[0], half_came.at[0])
    ids_copy.start()

    edge = lax.fori_loop(chunks - AHEAD, chunks, first_chunk, edge)
    row8 = lax.broadcasted_iota(jnp.int32, (8, LANES), 0)
    schur = edge[hours:]
    high = schur.astype(jnp.bfloat16).astype(jnp.float32)
    schur = jnp.where(row8 == 0, high, jnp.where(row8 == 1, schur - high, 0.0))
    blocks0[chip] = jnp.concatenate([edge[:hours], schur], axis=0).astype(jnp.bfloat16)
    send(blocks0, sems(1))

    @pl.loop(0, 64)
    def _(k):
        pltpu.make_async_copy(
            network_hbm.at[:, block_columns(k, c)],
            network.at[0:LANES, columns_of(k)],
            net_sems.at[0],
        ).start()
        to_partner(
            network_hbm.at[:, block_columns(k, 1 - c)],
            network.at[LANES : 2 * LANES, columns_of(k)],
            net_sems.at[1],
            net_sems.at[2],
        ).start()


    for dy in GROUPS:
        came(ids_all, sems(0), dy)
    ids_copy.wait()
    row256 = lax.broadcasted_iota(jnp.int32, (2 * LANES, LANES), 0)
    mine = row256 < LANES
    my_bus = jnp.where(
        mine, (chip * 2 + c) * LANES + row256, (chip * 2 + 1 - c) * LANES + row256 - LANES
    )

    @pl.loop(0, 64)
    def _(k):
        owned[:, columns_of(k)] = jnp.where(my_bus == ids_all[k], 1.0, 0.0).astype(jnp.bfloat16)

    hung = jnp.concatenate(
        [
            jnp.broadcast_to(my_ids[...], (LANES, LANES)).T,
            jnp.broadcast_to(their_ids[...], (LANES, LANES)).T,
        ],
        axis=0,
    )
    along = lax.broadcasted_iota(jnp.int32, (2 * LANES, LANES), 1)

    @pl.loop(0, 64)
    def _(k):
        buses = along + (k * 2 + c) * LANES
        chosen[:, columns_of(k)] = jnp.where(hung == buses, 1.0, 0.0).astype(jnp.bfloat16)

    totals = gather_dot(blocks0, sems(1), owned, theirs.at[0], ours.at[0])
    bus_schur = totals[hours : hours + 1] + totals[hours + 1 : hours + 2]
    totals = totals[:hours]

    def bus_phase(totals, mu, step, bus_now, p):
        right = bus_load_ref[...] + mu * jax.nn.sigmoid(-bus_now) - totals
        pivots = diagonal_ref[...] + mu + bus_schur
        blocks[p, chip] = (right / pivots).astype(jnp.bfloat16)
        send(blocks.at[p], sems(p + 2))
        if p == 0:
            bytes_of(network.at[0:LANES], net_sems.at[0])
            bytes_of(network.at[LANES : 2 * LANES], net_sems.at[2])
        coupled = gather_dot(
            blocks.at[p], sems(p + 2), network, theirs.at[p + 1], ours.at[p + 1]
        )
        second = (right - coupled) / pivots
        blocks[p + 1, chip] = second.astype(jnp.bfloat16)
        send(blocks.at[p + 1], sems(p + 3))
        return bus_now + step * second

    bus_now = bus_phase(totals, mu, step_ref[0], bus_state_ref[...], 0)

    at = step_ref[0] * gather_dot(blocks.at[1], sems(3), chosen, theirs.at[2], ours.at[2])

    mu = barrier_ref[1]
    step = step_ref[0]

    def second_chunk(k, edge):
        start = pl.multiple_of(k * CHUNK, CHUNK)
        rows = response_ref[pl.ds(start, CHUNK), :]
        here = pltpu.roll(at, lax.rem(LANES - start, LANES), 1)
        for j in range(CHUNK):
            f = start + j
            row = rows[j : j + 1, :]
            now = state[f] + (step * solved[f] - row * here[:, j : j + 1])
            state[f] = now
            residual = (load[f].astype(jnp.float32) + mu * jax.nn.sigmoid(-now)).astype(jnp.bfloat16)
            load[f] = residual
            scaled = residual.astype(jnp.float32) * row
            term = jnp.sum(scaled[:, :LANES] + scaled[:, LANES:], axis=1, keepdims=True)
            edge = jnp.where(lane[:hours] == f, term, edge)
        return edge

    edge = lax.fori_loop(0, chunks, second_chunk, jnp.zeros((hours, LANES), jnp.float32))
    blocks[2, chip] = edge.astype(jnp.bfloat16)
    send(blocks.at[2], sems(4))
    last_step = step_ref[1]

    @pl.loop(0, chunks)
    def _(k):
        for j in range(CHUNK):
            f = k * CHUNK + j
            product = jnp.dot(load[f], inverse[f], preferred_element_type=jnp.float32)
            y_ref[f] = state[f] + last_step * product

    totals = gather_dot(blocks.at[2], sems(4), owned, theirs.at[3], ours.at[3])
    bus_final_ref[...] = bus_phase(totals, mu, last_step, bus_now, 3)
    at_ref[...] = last_step * gather_dot(blocks.at[4], sems(6), chosen, theirs.at[5], ours.at[5])

    bytes_of(network.at[LANES : 2 * LANES], net_sems.at[1])
    others = pl.ds(0, len(OFFSETS))
    bytes_of(ids_all.at[others], sent.at[0])
    bytes_of(blocks0.at[others], sent.at[1])
    for p in range(5):
        bytes_of(blocks.at[p, others], sent.at[p + 2])


def last_kernel(y_ref, response_ref, at_ref, bus_ref, out_hbm, bus_final_ref, out, sem):
    feeders = y_ref.shape[0]
    bus_final_ref[...] = bus_ref[...]

    def copy(k):
        rows = pl.ds(k * CHUNK, CHUNK)
        return pltpu.make_async_copy(out.at[rows], out_hbm.at[rows], sem.at[k])

    for k in range(feeders // CHUNK):
        for f in range(k * CHUNK, (k + 1) * CHUNK):
            out[f] = y_ref[f] - response_ref[f : f + 1, :] * at_ref[:, f : f + 1]
        copy(k).start()
    for k in range(feeders // CHUNK):
        copy(k).wait()


def on_device(
    feeder_state,
    feeder_load,
    feeder_inverse,
    coupling,
    feeder_bus,
    bus_coupling,
    bus_diagonal,
    bus_load,
    bus_state,
    barrier,
    step_length,
):
    feeders, hours, nodes = feeder_state.shape
    owned, buses = bus_coupling.shape
    f32, bf16 = jnp.float32, jnp.bfloat16
    vmem, smem = pl.BlockSpec(memory_space=pltpu.VMEM), pl.BlockSpec(memory_space=pltpu.SMEM)
    hbm = pl.BlockSpec(memory_space=pltpu.HBM)
    chunks = feeders // CHUNK
    y, response, at, bus_last = pl.pallas_call(
        kernel,
        name="interior_point",
        out_shape=[
            pltpu.VMEM((feeders, hours, nodes), f32),
            pltpu.VMEM((feeders, nodes), f32),
            pltpu.VMEM((hours, LANES), f32),
            pltpu.VMEM((hours, owned), f32),
        ],
        in_specs=[hbm, hbm, hbm, vmem, vmem, hbm, vmem, vmem, vmem, smem, smem],
        out_specs=[vmem, vmem, vmem, vmem],
        scratch_shapes=[
            pltpu.VMEM((feeders, nodes, nodes), bf16),
            pltpu.VMEM((feeders, hours, nodes), f32),
            pltpu.VMEM((feeders, hours, nodes), bf16),
            pltpu.VMEM((feeders, hours, nodes), f32),
            pltpu.VMEM((2 * owned, buses // 2), bf16),
            pltpu.VMEM((2 * owned, 64 * LANES), bf16),
            pltpu.VMEM((2 * LANES, buses // 2), bf16),
            pltpu.VMEM((feeders, nodes), f32),
            pltpu.VMEM((64, hours + 8, LANES), bf16),
            pltpu.VMEM((5, 64, hours, LANES), bf16),
            pltpu.VMEM((64, 1, LANES), jnp.int32),
            pltpu.VMEM((1, LANES), jnp.int32),
            pltpu.VMEM((1, LANES), jnp.int32),
            pltpu.VMEM((6, hours + 8, LANES), f32),
            pltpu.VMEM((6, hours + 8, LANES), f32),
            pltpu.SemaphoreType.DMA((3, chunks)),
            pltpu.SemaphoreType.DMA((3,)),
            pltpu.SemaphoreType.DMA((7,)),
            pltpu.SemaphoreType.DMA((7, 4)),
            pltpu.SemaphoreType.DMA((7,)),
            pltpu.SemaphoreType.DMA((7,)),
        ],
        compiler_params=pltpu.CompilerParams(
            collective_id=0, has_side_effects=True, vmem_limit_bytes=64_430_080
        ),
    )(
        feeder_state,
        feeder_load,
        feeder_inverse,
        coupling,
        feeder_bus.reshape(1, feeders),
        bus_coupling,
        bus_diagonal.reshape(1, owned),
        bus_load,
        bus_state,
        barrier,
        step_length,
    )
    return pl.pallas_call(
        last_kernel,
        name="last_update",
        out_shape=[
            jax.ShapeDtypeStruct((feeders, hours, nodes), f32),
            jax.ShapeDtypeStruct((hours, owned), f32),
        ],
        in_specs=[vmem, vmem, vmem, vmem],
        out_specs=[hbm, vmem],
        scratch_shapes=[
            pltpu.VMEM((feeders, hours, nodes), f32),
            pltpu.SemaphoreType.DMA((chunks,)),
        ],
        compiler_params=pltpu.CompilerParams(vmem_limit_bytes=8 * 2**20),
    )(y, response, at, bus_last)


def solution(mesh):
    in_specs = (
        P(BOTH, None, None),
        P(BOTH, None, None),
        P(BOTH, None, None),
        P(BOTH, None),
        P(BOTH),
        P(BOTH, None),
        P(BOTH),
        P(None, BOTH),
        P(None, BOTH),
        P(),
        P(),
    )
    out_specs = (P(BOTH, None, None), P(None, BOTH))
    return jax.shard_map(
        on_device, mesh=mesh, in_specs=in_specs, out_specs=out_specs, check_vma=False
    )
```

time: 93.3 us -> 88.5 us (0.949)
  other arithmetic: 3.46 us -> 0 us
  local copies, waits for them, and re-layouts: 1.4 us -> 0 us
    sub x1 -> x0, other arithmetic: 3.46 us -> none  [on_device(): return (y - response[:, None, :] * at_feeder[:, :, None], bus_final)]
    pallas_call x1 -> x2, Pallas kernels: 87.5 us -> 87.7 us  [the longest x1 85.5 us: on_device(): pl.pallas_call(kernel, name='interior_point', out_shape=[pltpu.VMEM((feed...]
where the time goes in v2:
time: 88.5 us; the launch traced here: 88.3 us
  Pallas kernels  87.7 us (99%)
    pallas_call x1, Pallas kernels, on_device(): pl.pallas_call(kernel, name='interior_point', out_shape=[pltpu.VMEM((feed...  85.5 us
    pallas_call x1, Pallas kernels, on_device(): pl.pallas_call(last_kernel, name='last_update', out_shape=[jax.ShapeDtype...  2.19 us

profile of v2, /device:TPU:1, one launch (start us, length us, event | category | flops | bytes accessed | tf_op | source)
XLA Modules:
  0.0 88.3 jit_solution(10044604104401533942)
XLA Ops:
  0.6 85.5 %interior_point.1 = (f32[96,24,256]{2,1,0:T(8,128)S(1)}, f32[96,256]{1,0:T(8,128)S(1)}, f32[24,128]{1,0:T(8,128)S(1)}, f32[24,128]{1,0:T(8,128)S(1)}) custom-call(f32[96,24,256]{2,1,0:T(8,128)} %state_hbm.1, bf16[96,24,256]{2,1,0:T(8,128)(2,1)} %load_hbm.1, bf16[96,256,256]{2,1,0:T(8,128)(2,1)} %inverse_hbm.1, bf16[96,256]{1,0:T(8,128)(2,1)} %coupling_ref.1, ...), custom_call_target="tpu_custom_call" | custom-call | tf_op jit(solution)/shard_map/interior_point/pallas_call | solution.py:373
  86.1 2.2 %last_update.1 = (f32[96,24,256]{2,1,0:T(8,128)}, f32[24,128]{1,0:T(8,128)}) custom-call(f32[96,24,256]{2,1,0:T(8,128)S(1)} %get-tuple-element.6.y_ref, f32[96,256]{1,0:T(8,128)S(1)} %get-tuple-element.7.response_ref, f32[24,128]{1,0:T(8,128)S(1)} %get-tuple-element.8.at_ref, f32[24,128]{1,0:T(8,128)S(1)} %get-tuple-element.9.bus_ref), custom_call_target="tpu_custom_call" | custom-call | tf_op jit(solution)/shard_map/last_update/pallas_call | solution.py:423

commit v3 on v2

--- a/solution.py
+++ b/solution.py
@@ -86,19 +86,26 @@
     )
 
 
-def gather_dot(buf, sems, weights, theirs, ours):
+def gather_dot(buf, sems, weights, theirs, ours, turned=False):
     total = None
     for dy in GROUPS:
         plane = came(buf, sems, dy)
         columns = pl.ds(pl.multiple_of(plane * (16 * LANES), LANES), 16 * LANES)
-        part = lax.dot_general(
-            jnp.concatenate([buf[plane * 16 + k] for k in range(16)], axis=1),
-            weights[:, columns],
-            (((1,), (1,)), ((), ())),
-            preferred_element_type=jnp.float32,
-        )
+        here = jnp.concatenate([buf[plane * 16 + k] for k in range(16)], axis=1)
+        if turned:
+            part = jnp.dot(here, weights[columns, :], preferred_element_type=jnp.float32)
+        else:
+            part = lax.dot_general(
+                weights[:, columns],
+                here,
+                (((1,), (1,)), ((), ())),
+                preferred_element_type=jnp.float32,
+            )
         total = part if total is None else total + part
-    rows = total.shape[0]
+    rows = buf.shape[1]
+    if not turned:
+        empty = jnp.zeros((total.shape[0], LANES - rows), jnp.float32)
+        total = jnp.concatenate([total, empty], axis=1).T[:rows]
     theirs[0:rows] = total[:, LANES:]
     copy = to_partner(theirs.at[0:rows], ours.at[0:rows], sems[2], sems[3])
     copy.start()
@@ -137,6 +144,8 @@
     their_ids,
     theirs,
     ours,
+    owned_turned,
+    network_turned,
     load_sems,
     net_sems,
     sent,
@@ -254,23 +263,22 @@
     def _(k):
         owned[:, columns_of(k)] = jnp.where(my_bus == ids_all[k], 1.0, 0.0).astype(jnp.bfloat16)
 
-    hung = jnp.concatenate(
-        [
-            jnp.broadcast_to(my_ids[...], (LANES, LANES)).T,
-            jnp.broadcast_to(their_ids[...], (LANES, LANES)).T,
-        ],
-        axis=0,
-    )
-    along = lax.broadcasted_iota(jnp.int32, (2 * LANES, LANES), 1)
+    hung = jnp.concatenate([my_ids[...], their_ids[...]], axis=1)
+    down = lax.broadcasted_iota(jnp.int32, (LANES, 2 * LANES), 0)
 
     @pl.loop(0, 64)
     def _(k):
-        buses = along + (k * 2 + c) * LANES
-        chosen[:, columns_of(k)] = jnp.where(hung == buses, 1.0, 0.0).astype(jnp.bfloat16)
+        buses = down + (k * 2 + c) * LANES
+        chosen[columns_of(k), :] = jnp.where(hung == buses, 1.0, 0.0).astype(jnp.bfloat16)
 
     totals = gather_dot(blocks0, sems(1), owned, theirs.at[0], ours.at[0])
     bus_schur = totals[hours : hours + 1] + totals[hours + 1 : hours + 2]
     totals = totals[:hours]
+
+    def flip(src, dst):
+        @pl.loop(0, 64)
+        def _(k):
+            dst[columns_of(k), :] = src[:, columns_of(k)].T
 
     def bus_phase(totals, mu, step, bus_now, p):
         right = bus_load_ref[...] + mu * jax.nn.sigmoid(-bus_now) - totals
@@ -280,8 +288,14 @@
         if p == 0:
             bytes_of(network.at[0:LANES], net_sems.at[0])
             bytes_of(network.at[LANES : 2 * LANES], net_sems.at[2])
+            flip(owned, owned_turned)
         coupled = gather_dot(
-            blocks.at[p], sems(p + 2), network, theirs.at[p + 1], ours.at[p + 1]
+            blocks.at[p],
+            sems(p + 2),
+            network_turned if p else network,
+            theirs.at[p + 1],
+            ours.at[p + 1],
+            p > 0,
         )
         second = (right - coupled) / pivots
         blocks[p + 1, chip] = second.astype(jnp.bfloat16)
@@ -290,7 +304,8 @@
 
     bus_now = bus_phase(totals, mu, step_ref[0], bus_state_ref[...], 0)
 
-    at = step_ref[0] * gather_dot(blocks.at[1], sems(3), chosen, theirs.at[2], ours.at[2])
+    flip(network, network_turned)
+    at = step_ref[0] * gather_dot(blocks.at[1], sems(3), chosen, theirs.at[2], ours.at[2], True)
 
     mu = barrier_ref[1]
     step = step_ref[0]
@@ -323,9 +338,9 @@
             product = jnp.dot(load[f], inverse[f], preferred_element_type=jnp.float32)
             y_ref[f] = state[f] + last_step * product
 
-    totals = gather_dot(blocks.at[2], sems(4), owned, theirs.at[3], ours.at[3])
+    totals = gather_dot(blocks.at[2], sems(4), owned_turned, theirs.at[3], ours.at[3], True)
     bus_final_ref[...] = bus_phase(totals, mu, last_step, bus_now, 3)
-    at_ref[...] = last_step * gather_dot(blocks.at[4], sems(6), chosen, theirs.at[5], ours.at[5])
+    at_ref[...] = last_step * gather_dot(blocks.at[4], sems(6), chosen, theirs.at[5], ours.at[5], True)
 
     bytes_of(network.at[LANES : 2 * LANES], net_sems.at[1])
     others = pl.ds(0, len(OFFSETS))
@@ -388,7 +403,7 @@
             pltpu.VMEM((feeders, hours, nodes), f32),
             pltpu.VMEM((2 * owned, buses // 2), bf16),
             pltpu.VMEM((2 * owned, 64 * LANES), bf16),
-            pltpu.VMEM((2 * LANES, buses // 2), bf16),
+            pltpu.VMEM((buses // 2, 2 * LANES), bf16),
             pltpu.VMEM((feeders, nodes), f32),
             pltpu.VMEM((64, hours + 8, LANES), bf16),
             pltpu.VMEM((5, 64, hours, LANES), bf16),
@@ -397,6 +412,8 @@
             pltpu.VMEM((1, LANES), jnp.int32),
             pltpu.VMEM((6, hours + 8, LANES), f32),
             pltpu.VMEM((6, hours + 8, LANES), f32),
+            pltpu.VMEM((64 * LANES, 2 * owned), bf16),
+            pltpu.VMEM((buses // 2, 2 * owned), bf16),
             pltpu.SemaphoreType.DMA((3, chunks)),
             pltpu.SemaphoreType.DMA((3,)),
             pltpu.SemaphoreType.DMA((7,)),

time: 88.5 us -> 83.7 us (0.946)
  Pallas kernels: 87.7 us -> 82.9 us
    pallas_call x1, Pallas kernels: 85.5 us -> 80.7 us  [on_device(): pl.pallas_call(kernel, name='interior_point', out_shape=[pltpu.VMEM((feed...]
where the time goes in v3:
time: 83.7 us; the launch traced here: 83.5 us
  Pallas kernels  82.9 us (99%)
    pallas_call x1, Pallas kernels, on_device(): pl.pallas_call(kernel, name='interior_point', out_shape=[pltpu.VMEM((feed...  80.7 us
    pallas_call x1, Pallas kernels, on_device(): pl.pallas_call(last_kernel, name='last_update', out_shape=[jax.ShapeDtype...  2.19 us

profile of v3, /device:TPU:1, one launch (start us, length us, event | category | flops | bytes accessed | tf_op | source)
XLA Modules:
  0.0 83.5 jit_solution(12161103621331134142)
XLA Ops:
  0.6 80.7 %interior_point.1 = (f32[96,24,256]{2,1,0:T(8,128)S(1)}, f32[96,256]{1,0:T(8,128)S(1)}, f32[24,128]{1,0:T(8,128)S(1)}, f32[24,128]{1,0:T(8,128)S(1)}) custom-call(f32[96,24,256]{2,1,0:T(8,128)} %state_hbm.1, bf16[96,24,256]{2,1,0:T(8,128)(2,1)} %load_hbm.1, bf16[96,256,256]{2,1,0:T(8,128)(2,1)} %inverse_hbm.1, bf16[96,256]{1,0:T(8,128)(2,1)} %coupling_ref.1, ...), custom_call_target="tpu_custom_call" | custom-call | tf_op jit(solution)/shard_map/interior_point/pallas_call | solution.py:388
  81.3 2.2 %last_update.1 = (f32[96,24,256]{2,1,0:T(8,128)}, f32[24,128]{1,0:T(8,128)}) custom-call(f32[96,24,256]{2,1,0:T(8,128)S(1)} %get-tuple-element.6.y_ref, f32[96,256]{1,0:T(8,128)S(1)} %get-tuple-element.7.response_ref, f32[24,128]{1,0:T(8,128)S(1)} %get-tuple-element.8.at_ref, f32[24,128]{1,0:T(8,128)S(1)} %get-tuple-element.9.bus_ref), custom_call_target="tpu_custom_call" | custom-call | tf_op jit(solution)/shard_map/last_update/pallas_call | solution.py:440

commit v4 on v3

--- a/solution.py
+++ b/solution.py
@@ -89,8 +89,9 @@
 def gather_dot(buf, sems, weights, theirs, ours, turned=False):
     total = None
     for dy in GROUPS:
-        plane = came(buf, sems, dy)
-        columns = pl.ds(pl.multiple_of(plane * (16 * LANES), LANES), 16 * LANES)
+        came(buf, sems, dy)
+    for plane in range(4):
+        columns = slice(plane * 16 * LANES, (plane + 1) * 16 * LANES)
         here = jnp.concatenate([buf[plane * 16 + k] for k in range(16)], axis=1)
         if turned:
             part = jnp.dot(here, weights[columns, :], preferred_element_type=jnp.float32)
@@ -109,7 +110,7 @@
     theirs[0:rows] = total[:, LANES:]
     copy = to_partner(theirs.at[0:rows], ours.at[0:rows], sems[2], sems[3])
     copy.start()
-    copy.wait()
+    copy.wait_recv()
     return total[:, :LANES] + ours[0:rows]
 
 
@@ -346,6 +347,9 @@
     others = pl.ds(0, len(OFFSETS))
     bytes_of(ids_all.at[others], sent.at[0])
     bytes_of(blocks0.at[others], sent.at[1])
+    bytes_of(theirs.at[0], half_sent.at[1])
+    for p in range(1, 6):
+        bytes_of(theirs.at[p, 0:hours], half_sent.at[p + 1])
     for p in range(5):
         bytes_of(blocks.at[p, others], sent.at[p + 2])
 

time: 83.7 us -> 81.9 us (0.978)
  Pallas kernels: 82.9 us -> 81.1 us
    pallas_call x1, Pallas kernels: 80.7 us -> 78.9 us  [on_device(): pl.pallas_call(kernel, name='interior_point', out_shape=[pltpu.VMEM((feed...]
where the time goes in v4:
time: 81.9 us; the launch traced here: 81.8 us
  Pallas kernels  81.1 us (99%)
    pallas_call x1, Pallas kernels, on_device(): pl.pallas_call(kernel, name='interior_point', out_shape=[pltpu.VMEM((feed...  78.9 us
    pallas_call x1, Pallas kernels, on_device(): pl.pallas_call(last_kernel, name='last_update', out_shape=[jax.ShapeDtype...  2.19 us

profile of v4, /device:TPU:1, one launch (start us, length us, event | category | flops | bytes accessed | tf_op | source)
XLA Modules:
  0.0 81.8 jit_solution(14724967699627900497)
XLA Ops:
  0.6 78.9 %interior_point.1 = (f32[96,24,256]{2,1,0:T(8,128)S(1)}, f32[96,256]{1,0:T(8,128)S(1)}, f32[24,128]{1,0:T(8,128)S(1)}, f32[24,128]{1,0:T(8,128)S(1)}) custom-call(f32[96,24,256]{2,1,0:T(8,128)} %state_hbm.1, bf16[96,24,256]{2,1,0:T(8,128)(2,1)} %load_hbm.1, bf16[96,256,256]{2,1,0:T(8,128)(2,1)} %inverse_hbm.1, bf16[96,256]{1,0:T(8,128)(2,1)} %coupling_ref.1, ...), custom_call_target="tpu_custom_call" | custom-call | tf_op jit(solution)/shard_map/interior_point/pallas_call | solution.py:392
  79.6 2.2 %last_update.1 = (f32[96,24,256]{2,1,0:T(8,128)}, f32[24,128]{1,0:T(8,128)}) custom-call(f32[96,24,256]{2,1,0:T(8,128)S(1)} %get-tuple-element.6.y_ref, f32[96,256]{1,0:T(8,128)S(1)} %get-tuple-element.7.response_ref, f32[24,128]{1,0:T(8,128)S(1)} %get-tuple-element.8.at_ref, f32[24,128]{1,0:T(8,128)S(1)} %get-tuple-element.9.bus_ref), custom_call_target="tpu_custom_call" | custom-call | tf_op jit(solution)/shard_map/last_update/pallas_call | solution.py:444
